TPU v7x, 32 devices: a whole 2x2x4 slice. The times are simulated.
32 devices in a mesh: dp: 4 (over z), vocab: 8 (over y, x, core).
Axes of the slice: x: 2, y: 2, z: 4, core: 2. Of those that a mesh axis runs over, the one named last changes fastest.
Arguments:
- query_hidden: bfloat16 [128, 4096], P('dp', 'vocab'), may hold values from -6 to 6
- passage_hidden_rows: bfloat16 [384, 4096], P('dp', 'vocab'), may hold values from -6 to 6
- head_weight: bfloat16 [4096, 128256], P(None, ('dp', 'vocab')), may hold values from -0.09375 to 0.09375
- head_bias: bfloat16 [128256], P(('dp', 'vocab')), may hold values from -4 to 4
- query_mask: int32 [8, 16], P('dp'), may hold values from 0 to 1, as said below
- passage_mask: int32 [8, 48], P('dp'), may hold values from 0 to 1, as said below
- positives: int32 [8], P('dp'), may hold values from 0 to 7, as said below
Outputs:
- loss: float32 [], replicated
- query_grad: bfloat16 [128, 4096], P('dp', 'vocab')
- passage_grad: bfloat16 [384, 4096], P('dp', 'vocab')
Inputs may be any that keep to these rules, and one draw needn't show every extreme that they name: `query_mask`: each row holds 4 or more ones from its first token on, then zeros. `passage_mask`: each row holds 12 or more ones from its first token on, then zeros. `positives`: query i's positive is a passage of its own group: it lies in [(i // 2) * 2, (i // 2 + 1) * 2).
All inputs are finite; a program needn't handle non-finite values.
Results may differ from a plain program's by a relative error of at most 0.013.
Values may be sent and summed in bfloat16 or wider, within the bound.
A program may use at most 128 MiB of HBM per device.

v0:
```python
import functools

import jax
import jax.numpy as jnp
from jax import lax
from jax.experimental import pallas as pl
from jax.experimental.pallas import tpu as pltpu
from jax.sharding import PartitionSpec as P

logit_divisor = 50.0
loss_scale = 1048576.0
epsilon = 1e-06
HIGH = lax.Precision.HIGHEST


def segments(groups, seq_q, len_q, seq_p, len_p):
    rows = seq_q * len_q + seq_p * len_p
    found = []
    for g in range(groups):
        for i in range(seq_q):
            found.append((g * seq_q + i, g * rows + i * len_q, len_q))
        for j in range(seq_p):
            found.append(
                (groups * seq_q + g * seq_p + j, g * rows + seq_q * len_q + j * len_p, len_p)
            )
    return found


def forward_kernel(
    segs, cols, x_ref, w_ref, bias_ref, mask_ref, count_ref, sig_ref, rep_ref, inv_ref, gram_ref,
    xs, sums
):
    step = pl.program_id(0)
    blocks, rows, width = x_ref.shape
    tile = w_ref.shape[1]

    @pl.when(step == 0)
    def _():
        for v in range(blocks):
            xs[:, v * width : (v + 1) * width] = x_ref[v]
        gram_ref[...] = jnp.zeros_like(gram_ref)

    valid = lax.broadcasted_iota(jnp.int32, (1, tile), 1) < cols - step * tile
    logits = jnp.dot(xs[...], w_ref[...], preferred_element_type=jnp.float32)
    logits = logits + bias_ref[...].astype(jnp.float32)
    small = jnp.exp(-jnp.abs(logits))
    grown = 1.0 + small
    soft = jnp.maximum(logits, 0.0) + jnp.log(grown)
    keep = mask_ref[...]
    weight = keep * (1.0 + soft)
    share = keep * (jnp.where(logits >= 0.0, 1.0, small) / grown)
    sig_ref[...] = jnp.where(valid, share, 0.0).astype(sig_ref.dtype)
    for row, first, size in segs:
        sums[row : row + 1, :] = jnp.sum(weight[first : first + size], axis=0, keepdims=True)
    total = jnp.where(valid, sums[...], 1.0)
    rep = jnp.where(valid, jnp.log(total / count_ref[...]), 0.0)
    rep_ref[...] = rep
    inv_ref[...] = 1.0 / total
    gram_ref[...] += lax.dot_general(
        rep, rep, (((1,), (1,)), ((), ())), precision=HIGH, preferred_element_type=jnp.float32
    )


def contrast(gram, targets, queries):
    passages = gram.shape[0] - queries
    dots = gram[:queries, queries:]
    qq, pp = gram[:queries, :queries], gram[queries:, queries:]

    def eye(n):
        return (
            lax.broadcasted_iota(jnp.int32, (n, n), 0) == lax.broadcasted_iota(jnp.int32, (n, n), 1)
        ).astype(jnp.float32)

    q_col = jnp.sum(qq * eye(queries), axis=1, keepdims=True)
    p_row = jnp.sum(pp * eye(passages), axis=0, keepdims=True)
    scaling = logit_divisor / (jnp.sqrt(q_col + epsilon) * jnp.sqrt(p_row + epsilon))
    scores = dots * scaling
    exp_scores = jnp.exp(scores)
    exp_total = jnp.sum(exp_scores, axis=1, keepdims=True)
    onehot = (targets == lax.broadcasted_iota(jnp.int32, (queries, passages), 1)).astype(
        jnp.float32
    )
    losses = jnp.log(exp_total) - jnp.sum(onehot * scores, axis=1, keepdims=True)
    loss = jnp.sum(losses, axis=0, keepdims=True) / queries
    score_grad = (exp_scores / exp_total - onehot) * (loss_scale / queries)
    dots_grad = score_grad * scaling
    back = score_grad * scores
    q_coef = -jnp.sum(back, axis=1, keepdims=True) / (q_col + epsilon)
    p_coef = -jnp.sum(back, axis=0, keepdims=True) / (p_row + epsilon)
    return loss, dots_grad, q_coef, eye(passages) * p_coef


def backward_kernel(
    segs, queries, chunk, gram_ref, target_ref, rep_ref, inv_ref, sig_ref, w_ref, out_ref, loss_ref,
    dlog, scaled
):
    step = pl.program_id(0)
    cols = w_ref.shape[1]

    @pl.when(step == 0)
    def _():
        loss, dots_grad, q_coef, p_diag = contrast(gram_ref[...], target_ref[...], queries)
        loss_ref[...] = loss

        @pl.loop(0, dlog.shape[1] // chunk)
        def _(c):
            at = pl.ds(pl.multiple_of(c * chunk, chunk), chunk)
            rep = rep_ref[:, at]
            rep_q, rep_p = rep[:queries], rep[queries:]
            dot = functools.partial(
                lax.dot_general, precision=HIGH, preferred_element_type=jnp.float32
            )
            grad_q = dot(dots_grad, rep_p, (((1,), (0,)), ((), ()))) + q_coef * rep_q
            grad_p = dot(dots_grad, rep_q, (((0,), (0,)), ((), ()))) + dot(
                p_diag, rep_p, (((1,), (0,)), ((), ()))
            )
            inv = inv_ref[:, at]
            scaled[:queries] = grad_q * inv[:queries]
            scaled[queries:] = grad_p * inv[queries:]
            for row, first, size in segs:
                dlog[first : first + size, at] = (
                    sig_ref[first : first + size, at].astype(jnp.float32) * scaled[row : row + 1]
                ).astype(dlog.dtype)

    out_ref[0] = lax.dot_general(
        dlog[:, :cols], w_ref[...], (((1,), (1,)), ((), ())), preferred_element_type=jnp.float32
    ).astype(out_ref.dtype)


def compute_forward(x, head_weight, head_bias, keep, count, segs):
    blocks, rows, width = x.shape
    depth, cols = head_weight.shape
    tile = min(512, -(-cols // 128) * 128)
    tiles = -(-cols // tile)
    padded = tiles * tile
    block = tile if tile <= cols else cols
    if block != tile:
        tile, padded = cols, cols
    whole = lambda shape: pl.BlockSpec(shape, lambda i: (0,) * len(shape))
    seqs = count.shape[0]
    return pl.pallas_call(
        functools.partial(forward_kernel, segs, cols),
        grid=(tiles,),
        out_shape=(
            jax.ShapeDtypeStruct((rows, padded), jnp.bfloat16),
            jax.ShapeDtypeStruct((seqs, padded), jnp.float32),
            jax.ShapeDtypeStruct((seqs, padded), jnp.float32),
            jax.ShapeDtypeStruct((seqs, seqs), jnp.float32),
        ),
        in_specs=[
            whole(x.shape),
            pl.BlockSpec((depth, tile), lambda i: (0, i)),
            pl.BlockSpec((1, tile), lambda i: (0, i)),
            whole(keep.shape),
            whole(count.shape),
        ],
        out_specs=(
            pl.BlockSpec((rows, tile), lambda i: (0, i)),
            pl.BlockSpec((seqs, tile), lambda i: (0, i)),
            pl.BlockSpec((seqs, tile), lambda i: (0, i)),
            whole((seqs, seqs)),
        ),
        scratch_shapes=[
            pltpu.VMEM((rows, depth), jnp.bfloat16),
            pltpu.VMEM((seqs, tile), jnp.float32),
        ],
        compiler_params=pltpu.CompilerParams(vmem_limit_bytes=56 << 20),
    )(x, head_weight, head_bias.reshape(1, -1), keep, count)


def compute_backward(gram, targets, rep, inv, sig, head_weight, segs, blocks):
    depth, cols = head_weight.shape
    rows, padded = sig.shape
    seqs, queries = rep.shape[0], targets.shape[0]
    width = depth // blocks
    chunk = min(512, padded)
    whole = lambda shape: pl.BlockSpec(shape, lambda i: (0,) * len(shape))
    return pl.pallas_call(
        functools.partial(backward_kernel, segs, queries, chunk),
        grid=(blocks,),
        out_shape=(
            jax.ShapeDtypeStruct((blocks, rows, width), jnp.bfloat16),
            jax.ShapeDtypeStruct((1, 1), jnp.float32),
        ),
        in_specs=[
            whole(gram.shape),
            whole(targets.shape),
            whole(rep.shape),
            whole(inv.shape),
            whole(sig.shape),
            pl.BlockSpec((width, cols), lambda i: (i, 0)),
        ],
        out_specs=(pl.BlockSpec((1, rows, width), lambda i: (i, 0, 0)), whole((1, 1))),
        scratch_shapes=[
            pltpu.VMEM((rows, padded), jnp.bfloat16),
            pltpu.VMEM((seqs, chunk), jnp.float32),
        ],
        compiler_params=pltpu.CompilerParams(vmem_limit_bytes=56 << 20),
    )(gram, targets, rep, inv, sig, head_weight)


MESH = pl.DeviceIdType.MESH


def greet(peers):
    barrier = pltpu.get_barrier_semaphore()
    for peer in peers:
        pl.semaphore_signal(barrier, inc=1, device_id=peer, device_id_type=MESH)
    pl.semaphore_wait(barrier, len(peers))


def send(src, dst, send_sem, recv_sem, peer):
    return pltpu.make_async_remote_copy(
        src_ref=src,
        dst_ref=dst,
        send_sem=send_sem,
        recv_sem=recv_sem,
        device_id=peer,
        device_id_type=MESH,
    )


def places(groups, blocks):
    g, v = lax.axis_index("dp"), lax.axis_index("vocab")
    partner = v + 1 - 2 * lax.rem(v, 2)
    along_dp = [(lax.rem(g + k, groups), v) for k in range(1, groups)]
    along_vocab = [(g, lax.rem(v + 2 * j, blocks)) for j in range(1, blocks // 2)]
    return g, v, partner, along_dp, along_vocab


def gather_kernel(
    groups, blocks, own_ref, small_ref, out_ref, smalls_ref, local_sem, recv, recv_small, send_dp,
    send_small, send_vocab, send_pair
):
    g, v, partner, along_dp, along_vocab = places(groups, blocks)
    greet(along_dp + along_vocab + [(g, partner)])
    half = blocks // 2
    kept = pltpu.make_async_copy(own_ref, out_ref.at[v, g], local_sem.at[0])
    kept_small = pltpu.make_async_copy(small_ref, smalls_ref.at[g], local_sem.at[1])
    kept.start()
    kept_small.start()
    sent = []

    def go(src, vs, gs, sem, peer):
        copy = send(src, out_ref.at[vs, gs], sem, recv.at[vs, gs], peer)
        copy.start()
        sent.append(copy)

    def arrived(vs, gs):
        send(
            own_ref, out_ref.at[vs, gs], send_pair.at[0, 0], recv.at[vs, gs], (g, partner)
        ).wait_recv()

    for k, peer in enumerate(along_dp):
        go(own_ref, v, g, send_dp.at[k], peer)
    for k, peer in enumerate(along_dp):
        copy = send(small_ref, smalls_ref.at[g], send_small.at[k], recv_small.at[g], peer)
        copy.start()
        sent.append(copy)
    for k in range(groups):
        gs = lax.rem(g - k + groups, groups)
        src = own_ref
        if k:
            arrived(v, gs)
            src = out_ref.at[v, gs]
        for j, peer in enumerate(along_vocab):
            go(src, v, gs, send_vocab.at[k, j], peer)
        go(src, v, gs, send_pair.at[k, 0], (g, partner))
    for k in range(groups):
        gs = lax.rem(g - k + groups, groups)
        for j in range(1, half):
            vs = lax.rem(v - 2 * j + blocks, blocks)
            arrived(vs, gs)
            go(out_ref.at[vs, gs], vs, gs, send_pair.at[k, j], (g, partner))
    for k in range(groups):
        gs = lax.rem(g - k + groups, groups)
        for j in range(half):
            arrived(lax.rem(partner - 2 * j + blocks, blocks), gs)
        if k:
            send(
                small_ref, smalls_ref.at[gs], send_small.at[0], recv_small.at[gs], (g, partner)
            ).wait_recv()
    for copy in sent:
        copy.wait_send()
    kept.wait()
    kept_small.wait()


def gather_all(own, small, groups, blocks):
    half, dma = blocks // 2, pltpu.SemaphoreType.DMA
    anywhere = pl.BlockSpec(memory_space=pl.ANY)
    return pl.pallas_call(
        functools.partial(gather_kernel, groups, blocks),
        out_shape=(
            jax.ShapeDtypeStruct((blocks, groups) + own.shape, own.dtype),
            jax.ShapeDtypeStruct((groups,) + small.shape, small.dtype),
        ),
        in_specs=[anywhere, anywhere],
        out_specs=(anywhere, anywhere),
        scratch_shapes=[
            dma((2,)),
            dma((blocks, groups)),
            dma((groups,)),
            dma((max(groups - 1, 1),)),
            dma((max(groups - 1, 1),)),
            dma((groups, max(half - 1, 1))),
            dma((groups, half)),
        ],
        compiler_params=pltpu.CompilerParams(collective_id=0, has_side_effects=True),
    )(own, small)


def total_kernel(groups, blocks, part_ref, out_ref, buf, local_sem, recv_v, send_v, recv_g, send_g):
    g, v = lax.axis_index("dp"), lax.axis_index("vocab")
    along_dp = [(lax.rem(g + k, groups), v) for k in range(1, groups)]
    along_vocab = [(g, lax.rem(v + j, blocks)) for j in range(1, blocks)]
    greet(along_dp + along_vocab)
    kept = pltpu.make_async_copy(part_ref, buf.at[g, v], local_sem.at[0])
    kept.start()
    sent = []
    for j, peer in enumerate(along_vocab):
        copy = send(part_ref, buf.at[g, v], send_v.at[j], recv_v.at[v], peer)
        copy.start()
        sent.append(copy)
    kept.wait()
    for j in range(1, blocks):
        vs = lax.rem(v - j + blocks, blocks)
        send(part_ref, buf.at[g, vs], send_v.at[0], recv_v.at[vs], (g, vs)).wait_recv()
    for k, peer in enumerate(along_dp):
        copy = send(buf.at[g], buf.at[g], send_g.at[k], recv_g.at[g], peer)
        copy.start()
        sent.append(copy)
    for k in range(1, groups):
        gs = lax.rem(g - k + groups, groups)
        send(buf.at[gs], buf.at[gs], send_g.at[0], recv_g.at[gs], (gs, v)).wait_recv()
    total = jnp.zeros(out_ref.shape, jnp.float32)
    for a in range(groups):
        for b in range(blocks):
            total = total + buf[a, b]
    out_ref[...] = total
    for copy in sent:
        copy.wait_send()


def total_all(part, groups, blocks):
    dma = pltpu.SemaphoreType.DMA
    inside = pl.BlockSpec(memory_space=pltpu.VMEM)
    return pl.pallas_call(
        functools.partial(total_kernel, groups, blocks),
        out_shape=jax.ShapeDtypeStruct(part.shape, part.dtype),
        in_specs=[inside],
        out_specs=inside,
        scratch_shapes=[
            pltpu.VMEM((groups, blocks) + part.shape, jnp.float32),
            dma((1,)),
            dma((blocks,)),
            dma((max(blocks - 1, 1),)),
            dma((groups,)),
            dma((max(groups - 1, 1),)),
        ],
        compiler_params=pltpu.CompilerParams(collective_id=1, has_side_effects=True),
    )(part)


def scatter_kernel(
    groups, blocks, rows_q, a_ref, q_ref, p_ref, pair, pooled, peers, turned, last, recv_pair,
    send_pair, recv_vocab, send_vocab, recv_dp, send_dp
):
    g, v, partner, along_dp, along_vocab = places(groups, blocks)
    greet(along_dp + along_vocab + [(g, partner)])
    half = blocks // 2
    rows = a_ref.shape[1] // groups
    sent = []

    def go(src, dst, send_sem, recv_sem, peer):
        copy = send(src, dst, send_sem, recv_sem, peer)
        copy.start()
        sent.append(copy)

    order = list(range(1, half)) + [0]
    for j in order:
        w = lax.rem(partner + 2 * j, blocks)
        go(a_ref.at[w], pair.at[w // 2], send_pair.at[j], recv_pair.at[w // 2], (g, partner))
    for j in order:
        w = lax.rem(v + 2 * j, blocks)
        at = w // 2
        send(
            a_ref.at[w], pair.at[at], send_pair.at[0], recv_pair.at[at], (g, partner)
        ).wait_recv()
        pooled[at] = (
            a_ref[w].astype(jnp.float32) + pair[at].astype(jnp.float32)
        ).astype(pooled.dtype)
        if j:
            go(
                pooled.at[at],
                peers.at[v // 2],
                send_vocab.at[j - 1],
                recv_vocab.at[v // 2],
                along_vocab[j - 1],
            )
    for j in range(1, half):
        at = lax.rem(v - 2 * j + blocks, blocks) // 2
        send(
            pooled.at[at], peers.at[at], send_vocab.at[0], recv_vocab.at[at], (g, partner)
        ).wait_recv()

    def summed(gs):
        part = pl.ds(pl.multiple_of(gs * rows, rows), rows)
        out = pooled[v // 2, part].astype(jnp.float32)
        for j in range(1, half):
            at = lax.rem(v - 2 * j + blocks, blocks) // 2
            out = out + peers[at, part].astype(jnp.float32)
        return out

    for k, peer in enumerate(along_dp):
        turned[k] = summed(peer[0]).astype(turned.dtype)
        go(turned.at[k], last.at[g], send_dp.at[k], recv_dp.at[g], peer)
    out = summed(g)
    for k in range(1, groups):
        gs = lax.rem(g - k + groups, groups)
        send(turned.at[0], last.at[gs], send_dp.at[0], recv_dp.at[gs], (gs, v)).wait_recv()
        out = out + last[gs].astype(jnp.float32)
    q_ref[...] = out[:rows_q].astype(q_ref.dtype)
    p_ref[...] = out[rows_q:].astype(p_ref.dtype)
    for copy in sent:
        copy.wait_send()


def scatter_all(parts, groups, rows_q):
    blocks, tokens, width = parts.shape
    half, rows, dma = blocks // 2, tokens // groups, pltpu.SemaphoreType.DMA
    inside = pl.BlockSpec(memory_space=pltpu.VMEM)
    block = pltpu.VMEM((half, tokens, width), parts.dtype)
    return pl.pallas_call(
        functools.partial(scatter_kernel, groups, blocks, rows_q),
        out_shape=(
            jax.ShapeDtypeStruct((rows_q, width), parts.dtype),
            jax.ShapeDtypeStruct((rows - rows_q, width), parts.dtype),
        ),
        in_specs=[inside],
        out_specs=(inside, inside),
        scratch_shapes=[
            block,
            block,
            block,
            pltpu.VMEM((max(groups - 1, 1), rows, width), parts.dtype),
            pltpu.VMEM((groups, rows, width), parts.dtype),
            dma((half,)),
            dma((half,)),
            dma((half,)),
            dma((max(half - 1, 1),)),
            dma((groups,)),
            dma((max(groups - 1, 1),)),
        ],
        compiler_params=pltpu.CompilerParams(
            collective_id=2, has_side_effects=True, vmem_limit_bytes=48 << 20
        ),
    )(parts)


def shards(
    query_hidden, passage_hidden_rows, head_weight, head_bias, query_mask, passage_mask, positives
):
    groups, blocks = lax.axis_size("dp"), lax.axis_size("vocab")
    seq_q, len_q = query_mask.shape
    seq_p, len_p = passage_mask.shape
    rows_q = seq_q * len_q
    rows, width = rows_q + seq_p * len_p, query_hidden.shape[1]
    segs = segments(groups, seq_q, len_q, seq_p, len_p)

    own = jnp.concatenate((query_hidden, passage_hidden_rows), 0)
    small = jnp.concatenate((query_mask.reshape(-1), passage_mask.reshape(-1), positives))
    lanes = 128
    held = -(-small.shape[0] // (8 * lanes)) * 8 * lanes
    ints = small.shape[0]
    small = jnp.pad(small, (0, held - ints)).reshape(-1, lanes)
    x, small = gather_all(own, small, groups, blocks)
    x = x.reshape(blocks, groups * rows, width)
    small = small.reshape(groups, held)[:, :ints]
    targets = small[:, rows:].reshape(-1, 1)
    keep = small[:, :rows].astype(jnp.float32)
    count = jnp.concatenate(
        (
            jnp.sum(keep[:, :rows_q].reshape(-1, len_q), axis=1),
            jnp.sum(keep[:, rows_q:].reshape(-1, len_p), axis=1),
        )
    )[:, None]
    sig, rep, inv, gram = compute_forward(
        x, head_weight, head_bias, keep.reshape(-1, 1), count, segs
    )
    gram = total_all(gram, groups, blocks)
    grads, loss = compute_backward(gram, targets, rep, inv, sig, head_weight, segs, blocks)
    query_grad, passage_grad = scatter_all(grads, groups, rows_q)
    return (loss[0, 0], query_grad, passage_grad)


def solution(mesh):
    placed = (
        P("dp", "vocab"),
        P("dp", "vocab"),
        P(None, ("dp", "vocab")),
        P(("dp", "vocab")),
        P("dp", None),
        P("dp", None),
        P("dp"),
    )
    return jax.shard_map(
        shards,
        mesh=mesh,
        in_specs=placed,
        out_specs=(P(), P("dp", "vocab"), P("dp", "vocab")),
        check_vma=False,
    )
```

profile of v0, /device:TPU:0, one launch (start us, length us, event | category | flops | bytes accessed | tf_op | source)
XLA Modules:
  0.0 197.3 jit_solution(3362848954726338581)
XLA Ops:
  0.6 0.8 reshape.36
  1.4 0.8 reshape.37
  2.1 0.7 pad_add_fusion
  2.9 0.6 pad_bitcast_fusion.small_ref
  3.5 1.3 reshape.40.bias_ref
  4.8 1.5 pad_maximum_fusion.own_ref
  6.3 32.1 %shard_map.94 = (bf16[8,4,128,512]{3,2,1,0:T(8,128)(2,1)}, s32[4,8,128]{2,1,0:T(8,128)}) custom-call(bf16[128,512]{1,0:T(8,128)(2,1)} %pad_maximum_fusion.own_ref, s32[8,128]{1,0:T(8,128)} %pad_bitcast_fusion.small_ref), custom_call_target="tpu_custom_call" | custom-call | tf_op jit(solution)/shard_map/pallas_call | solution.py:292
  38.4 0.7 copy.21
  39.1 0.7 reshape.46.target_ref
  39.9 0.1 reshape.44
  40.0 0.1 reduce_sum.19
  40.1 0.1 reshape.43
  40.2 0.1 reduce_sum.18
  40.3 0.1 maximum_bitcast_fusion
  40.4 0.7 copy.16.count_ref
  41.0 0.9 copy.15.mask_ref
  41.9 41.3 %copy.14.w_ref = bf16[4096,4008]{1,0:T(8,128)(2,1)} copy(bf16[4096,4008]{0,1:T(8,128)(2,1)} %param.9) | data formatting | bytes 65667072 | tf_op args[2]
  83.2 29.8 %shard_map.95 = (bf16[512,4096]{1,0:T(8,128)(2,1)}, f32[16,4096]{1,0:T(8,128)}, f32[16,4096]{1,0:T(8,128)}, f32[16,16]{1,0:T(8,128)}) custom-call(bf16[8,512,512]{2,1,0:T(8,128)(2,1)} %bitcast.12, bf16[4096,4008]{1,0:T(8,128)(2,1)} %copy.14.w_ref, bf16[1,4008]{1,0:T(2,128)(2,1)} %reshape.40.bias_ref, f32[512,1]{1,0:T(8,128)} %copy.15.mask_ref, ...), custom_call_target="tpu_custom_call" | custom-call | tf_op jit(solution)/shard_map/pallas_call | solution.py:141
  112.9 14.3 %shard_map.96.gram_ref = f32[16,16]{1,0:T(8,128)} custom-call(f32[16,16]{1,0:T(8,128)} %get-tuple-element.15.part_ref), custom_call_target="tpu_custom_call" | custom-call | tf_op jit(solution)/shard_map/pallas_call | solution.py:348
  127.2 26.8 %shard_map.97 = (bf16[8,512,512]{2,1,0:T(8,128)(2,1)}, f32[1,1]{1,0:T(1,128)}) custom-call(f32[16,16]{1,0:T(8,128)} %shard_map.96.gram_ref, s32[8,1]{1,0:T(8,128)} %reshape.46.target_ref, f32[16,4096]{1,0:T(8,128)} %get-tuple-element.16.rep_ref, f32[16,4096]{1,0:T(8,128)} %get-tuple-element.17.inv_ref, bf16[512,4096]{1,0:T(8,128)(2,1)} %get-tuple-element.18.sig_ref, ...), custom_call_target="tpu_custom_call" | custom-call | tf_op jit(solution)/shard_map/pallas_call | solution.py:178
  154.0 2.2 %copy-done = bf16[8,512,512]{2,1,0:T(8,128)(2,1)S(1)} copy-done((bf16[8,512,512]{2,1,0:T(8,128)(2,1)S(1)}, bf16[8,512,512]{2,1,0:T(8,128)(2,1)}, u32[]{:S(2)}) %copy-start) | copy-done | bytes 4194328
  156.2 39.8 %shard_map.98 = (bf16[32,512]{1,0:T(8,128)(2,1)S(1)}, bf16[96,512]{1,0:T(8,128)(2,1)S(1)}) custom-call(bf16[8,512,512]{2,1,0:T(8,128)(2,1)S(1)} %copy-done), custom_call_target="tpu_custom_call" | custom-call | tf_op jit(solution)/shard_map/pallas_call | solution.py:434
  196.0 0.6 copy.24
  196.6 0.6 copy.25
  (4 shorter events, 0.1 us)
Async XLA Ops:
  154.0 2.2 %copy-start = (bf16[8,512,512]{2,1,0:T(8,128)(2,1)S(1)}, bf16[8,512,512]{2,1,0:T(8,128)(2,1)}, u32[]{:S(2)}) copy-start(bf16[8,512,512]{2,1,0:T(8,128)(2,1)} %get-tuple-element.20.a_ref) | copy-start | bytes 12582916
where the time goes:
time: 199 us; the launch traced here: 197 us
  Pallas kernels  143 us (72%)
  local copies, waits for them, and re-layouts  51.3 us (26%)
  other arithmetic  2.59 us (1%)
    unnamed x6, local copies, waits for them, and re-layouts  45.4 us
    pallas_call x1, Pallas kernels, scatter_all(): pl.pallas_call(functools.partial(scatter_kernel, groups, blocks, rows_q),...  39.8 us
    pallas_call x1, Pallas kernels, gather_all(): pl.pallas_call(functools.partial(gather_kernel, groups, blocks), out_shap...  32.1 us
    pallas_call x1, Pallas kernels, compute_forward(): pl.pallas_call(functools.partial(forward_kernel, segs, cols), grid=(tiles...  29.8 us
    pallas_call x1, Pallas kernels, compute_backward(): pl.pallas_call(functools.partial(backward_kernel, segs, queries, chunk),...  26.8 us
    pallas_call x1, Pallas kernels, total_all(): pl.pallas_call(functools.partial(total_kernel, groups, blocks), out_shape...  14.3 us

commit v1 on v0

v1 whole, which is shorter than its diff:
```python
import functools

import jax
import jax.numpy as jnp
from jax import lax
from jax.experimental import pallas as pl
from jax.experimental.pallas import tpu as pltpu
from jax.sharding import PartitionSpec as P

logit_divisor = 50.0
loss_scale = 1048576.0
epsilon = 1e-06
lanes = 128
MESH = pl.DeviceIdType.MESH


def aligned(at, step):
    return at if isinstance(at, int) else pl.multiple_of(at, step)


def contrast(stats, targets, n):
    dots = stats[:, :n]
    eye = lax.broadcasted_iota(jnp.int32, (n, n), 0) == lax.broadcasted_iota(jnp.int32, (n, n), 1)
    q_row = jnp.sum(jnp.where(eye, stats[:, n : n + 1], 0.0), axis=0, keepdims=True)
    p_col = stats[:, n + 1 : n + 2]
    scaling = logit_divisor / (jnp.sqrt(q_row + epsilon) * jnp.sqrt(p_col + epsilon))
    scores = dots * scaling
    exp_scores = jnp.exp(scores)
    exp_total = jnp.sum(exp_scores, axis=0, keepdims=True)
    index = lax.broadcasted_iota(jnp.int32, (n, n), 0).astype(jnp.float32)
    onehot = (targets == index).astype(jnp.float32)
    losses = jnp.log(exp_total) - jnp.sum(onehot * scores, axis=0, keepdims=True)
    loss = jnp.sum(losses, axis=1, keepdims=True) / n
    score_grad = (exp_scores / exp_total - onehot) * (loss_scale / n)
    dots_grad = score_grad * scaling
    back = score_grad * scores
    q_coef = -jnp.sum(back, axis=0, keepdims=True) / (q_row + epsilon)
    p_coef = -jnp.sum(back, axis=1, keepdims=True) / (p_col + epsilon)

    def column(row):
        return jnp.sum(jnp.where(eye, row, 0.0), axis=1, keepdims=True)

    for_q = [column(dots_grad[j : j + 1]) for j in range(n)]
    for_p = [dots_grad[:, i : i + 1] for i in range(n)]
    return loss, for_q, for_p, column(q_coef), p_coef


def head_kernel(
    groups, blocks, seq_q, len_q, seq_p, len_p, cols, tile, unroll,
    q_ref, p_ref, w_ref, bias_ref, qm_ref, pm_ref, pos_ref, loss_ref, qo_ref, po_ref,
    x, wv, sig, keep, sums, rep, inv, acc, small, smalls, counts, goal, stat_v, stat_g,
    away, pair, mine, pooled, relayed, froms, turned, last,
    w_sem, own_sem, z_send, small_send, small_recv, x_send, x_recv,
    sv_send, sv_recv, sg_send, sg_recv, pair_send, pair_recv, plane_send, relay_recv, from_recv,
    last_send, last_recv,
):
    g, v = lax.axis_index("dp"), lax.axis_index("vocab")
    chip, core = lax.div(v, 2), lax.rem(v, 2)
    partner = v + 1 - 2 * core
    half = blocks // 2
    tree = half == 4
    rows_q = seq_q * len_q
    rows, width = rows_q + seq_p * len_p, q_ref.shape[1]
    queries, tiles = groups * seq_q, x.shape[1] and sig.shape[1] // tile
    seqs = seq_q + seq_p

    def to_chip(r):
        if tree:
            return lax.rem(lax.div(chip, 2) + r // 2, 2) * 2 + lax.rem(chip + r % 2, 2)
        return lax.rem(chip + r, half)

    def from_chip(r):
        return to_chip(r) if tree else lax.rem(chip + half - r, half)

    def vocab_of(c):
        return c * 2 + core

    started = []

    def go(src, dst, send_sem, recv_sem, peer, like):
        pltpu.make_async_remote_copy(
            src_ref=src, dst_ref=dst, send_sem=send_sem[0].at[send_sem[1:]], recv_sem=recv_sem,
            device_id=peer, device_id_type=MESH,
        ).start()
        started.append((send_sem, like))

    def arrived(dst, recv_sem, peer):
        pltpu.make_async_remote_copy(
            src_ref=dst, dst_ref=dst, send_sem=z_send.at[0], recv_sem=recv_sem,
            device_id=peer, device_id_type=MESH,
        ).wait_recv()

    def drain():
        for send_sem, like in started:
            pltpu.make_async_remote_copy(
                src_ref=like[0].at[like[1:]], dst_ref=like[0].at[like[1:]],
                send_sem=send_sem[0].at[send_sem[1:]], recv_sem=z_send.at[0],
                device_id=(g, partner), device_id_type=MESH,
            ).wait_send()
        started.clear()

    loads = []
    stored = w_ref.shape[0]
    for t in range(tiles):
        n = min(tile, stored - t * tile)
        at = pl.ds(t * tile, n)
        loads.append(pltpu.make_async_copy(w_ref.at[at], wv.at[at], w_sem.at[t]))

    def block(vs, gs, part=None):
        n = rows if part is None else rows // 2
        at = gs * rows if part is None else gs * rows + part * n
        return x.at[
            pl.ds(aligned(at, n), n), pl.ds(aligned(vs * width, width), width)
        ]

    full = (x, pl.ds(0, rows), pl.ds(0, width))
    part_of = (x, pl.ds(0, rows // 2), pl.ds(0, width))
    own_cols = pl.ds(aligned(v * width, width), width)
    own_q = pltpu.make_async_copy(
        q_ref, x.at[pl.ds(aligned(g * rows, rows), rows_q), own_cols], own_sem.at[0]
    )
    own_p = pltpu.make_async_copy(
        p_ref,
        x.at[pl.ds(aligned(g * rows + rows_q, rows_q), rows - rows_q), own_cols],
        own_sem.at[1],
    )
    own_q.start()
    own_p.start()
    for load in loads:
        load.start()

    along_dp = [(lax.rem(g + k, groups), v) for k in range(1, groups)]
    along_vocab = [(g, lax.rem(v + k, blocks)) for k in range(1, blocks)]
    barrier = pltpu.get_barrier_semaphore()
    for peer in along_dp + along_vocab:
        pl.semaphore_signal(barrier, inc=1, device_id=peer, device_id_type=MESH)

    small[...] = jnp.zeros(small.shape, small.dtype)
    small[:seq_q, :len_q] = qm_ref[...]
    small[seq_q:seqs, :len_p] = pm_ref[...]
    lane = lax.broadcasted_iota(jnp.int32, (1, lanes), 1)
    row = jnp.zeros((1, lanes), jnp.int32)
    for i in range(seq_q):
        row = jnp.where(lane == i, pos_ref[i], row)
    small[seqs : seqs + 1] = row
    smalls[g] = small[...]
    pl.semaphore_wait(barrier, len(along_dp + along_vocab))

    pairs = groups // 2
    order = [g, g + 1 - 2 * lax.rem(g, 2)]
    bases = [lax.rem(lax.div(g, 2) + k, pairs) * 2 for k in range(pairs)]
    for base in bases[1:]:
        order += [base, base + 1]

    direct = [1, 2] if tree else list(range(1, half))

    def fan(n):
        gs = order[n]
        for k, r in enumerate(direct):
            vs = vocab_of(to_chip(r))
            go(block(v, gs), block(v, gs), (x_send, n, k), x_recv.at[v, gs, 0], (g, vs), full)
        sem = (x_send, n, half)
        go(block(v, gs), block(v, gs), sem, x_recv.at[v, gs, 0], (g, partner), full)

    def relay(n):
        gs = order[n]
        for k, r in enumerate(direct):
            vs = vocab_of(from_chip(r))
            arrived(block(vs, gs), x_recv.at[vs, gs, 0], (g, partner))
            if tree:
                to = (g, vocab_of(to_chip(3 - r)))
                part = block(vs, gs, k)
                go(part, part, (x_send, n, half + 1 + k), x_recv.at[vs, gs, k], to, part_of)
            go(
                block(vs, gs), block(vs, gs), (x_send, n, len(direct) + 3 + half + k),
                x_recv.at[vs, gs, 0], (g, partner), full,
            )

    def corner(n):
        if not tree:
            return
        gs, vs = order[n], vocab_of(to_chip(3))
        for k in range(2):
            part = block(vs, gs, k)
            arrived(part, x_recv.at[vs, gs, k], (g, partner))
            sem = (x_send, n, half + 3 + k)
            go(part, part, sem, x_recv.at[vs, gs, k], (g, partner), part_of)

    def settled(n):
        gs = order[n]
        for r in range(half):
            vs = from_chip(r) * 2 + 1 - core
            if tree and r == 3:
                for k in range(2):
                    arrived(block(vs, gs, k), x_recv.at[vs, gs, k], (g, partner))
            else:
                arrived(block(vs, gs), x_recv.at[vs, gs, 0], (g, partner))

    own_q.wait()
    own_p.wait()
    for n in range(1, groups):
        go(block(v, g), block(v, g), (z_send, n - 1), x_recv.at[v, g, 0], (order[n], v), full)
        if n == 1:
            fan(0)
    for n in range(1, groups):
        sem = (small_send, n - 1)
        go(smalls.at[g], smalls.at[g], sem, small_recv.at[g], (order[n], v), (smalls, 0))

    def reach(n):
        arrived(block(v, order[n]), x_recv.at[v, order[n], 0], (g, partner))
        fan(n)

    reach(1)
    relay(0)
    relay(1)
    for n in range(2, groups):
        reach(n)

    for n in range(1, groups):
        gs = order[n]
        arrived(smalls.at[gs], small_recv.at[gs], (g, partner))
    aim = jnp.zeros((1, lanes), jnp.float32)
    for a in range(groups):
        ints = smalls[a].astype(jnp.float32)
        ones = jnp.sum(ints, axis=1, keepdims=True)
        first = a * rows
        for s in range(seqs):
            size = len_q if s < seq_q else len_p
            held = lax.broadcasted_iota(jnp.int32, (size, lanes), 0).astype(jnp.float32)
            keep[first : first + size] = (held < ones[s : s + 1]).astype(jnp.float32)
            first += size
            at = a * seq_q + s if s < seq_q else queries + a * seq_p + s - seq_q
            counts[at : at + 1] = jnp.broadcast_to(ones[s : s + 1], (1, lanes))
        for i in range(seq_q):
            value = jnp.sum(
                jnp.where(lane == i, ints[seqs : seqs + 1], 0.0), axis=1, keepdims=True
            )
            aim = jnp.where(lane == a * seq_q + i, value, aim)
    goal[...] = aim

    corner(0)
    corner(1)
    settled(0)
    settled(1)

    some = 2 * rows

    def product(base, t, slot):
        acc[slot] = lax.dot_general(
            x[pl.ds(aligned(base * rows, some), some)],
            wv[pl.ds(aligned(t * tile, tile), tile)],
            (((1,), (1,)), ((), ())),
            preferred_element_type=jnp.float32,
        )

    def pool(base, t, slot):
        at = pl.ds(aligned(t * tile, tile), tile)
        bias = bias_ref[:, at]
        for m in range(2):
            first = m * rows
            for s in range(seqs):
                size = len_q if s < seq_q else len_p
                step = 16 if size % 16 == 0 else size
                total = None
                for r in range(first, first + size, step):
                    logits = acc[slot, r : r + step] + bias
                    low = jnp.exp(-jnp.abs(logits))
                    grown = 1.0 + low
                    soft = jnp.maximum(logits, 0.0) + jnp.log(grown)
                    place = pl.ds(aligned(base * rows + r, step), step)
                    kept = jnp.concatenate([keep[place]] * (tile // lanes), axis=1)
                    weight = kept * (1.0 + soft)
                    share = kept * (jnp.where(logits >= 0.0, 1.0, low) / grown)
                    sig[place, at] = share.astype(sig.dtype)
                    total = weight if total is None else total + weight
                sums[base + m, s : s + 1, at] = jnp.sum(total, axis=0, keepdims=True)
                first += size

    rounds = tiles // unroll
    for k, base in enumerate(bases):
        events = []
        if k + 1 < pairs:
            a, b = 2 * k + 2, 2 * k + 3
            events = [(relay, a), (relay, b), (corner, a), (corner, b)]

        @pl.loop(0, rounds)
        def _(i):
            if k == 0:
                for r in range(rounds):

                    @pl.when(i == r)
                    def _():
                        for load in loads[r * unroll : (r + 1) * unroll]:
                            load.wait()

            for u in range(unroll):
                t = i * unroll + u
                product(base, t, u)
                if unroll > 1:
                    pool(base, jnp.maximum(t - 1, 0), (u - 1) % unroll)
                else:
                    pool(base, t, u)
            for e, (event, n) in enumerate(events):

                @pl.when(i == min(e, rounds - 1))
                def _():
                    event(n)

        if unroll > 1:
            pool(base, tiles - 1, unroll - 1)
        if k + 1 < pairs:
            settled(2 * k + 2)
            settled(2 * k + 3)

    parts = tile // lanes
    fold = lambda y: sum(y[:, n * lanes : (n + 1) * lanes] for n in range(parts))
    cross = [None] * queries
    squares = [None, None]
    plus = lambda a, b: b if a is None else a + b
    for t in range(tiles):
        at = slice(t * tile, (t + 1) * tile)
        valid = lax.broadcasted_iota(jnp.int32, (1, tile), 1) < cols - t * tile
        reps = []
        for kind, (low, high) in enumerate(((0, seq_q), (seq_q, seqs))):
            total = jnp.concatenate([sums[a, low:high, at] for a in range(groups)], axis=0)
            total = jnp.where(valid, total, 1.0)
            part = slice(kind * queries, (kind + 1) * queries)
            count = jnp.concatenate([counts[part]] * parts, axis=1)
            value = jnp.where(valid, jnp.log(total / count), 0.0)
            rep[part, at] = value
            inv[part, at] = 1.0 / total
            reps.append(value)
            squares[kind] = plus(squares[kind], fold(value * value))
        for i in range(queries):
            cross[i] = plus(cross[i], fold(reps[0][i : i + 1] * reps[1]))
    wide = lax.broadcasted_iota(jnp.int32, (queries, lanes), 1)
    stats = jnp.zeros((queries, lanes), jnp.float32)
    for i, piece in enumerate(cross + squares):
        stats = jnp.where(wide == i, jnp.sum(piece, axis=1, keepdims=True), stats)

    stat_v[v] = stats
    for k, peer in enumerate(along_vocab):
        go(stat_v.at[v], stat_v.at[v], (sv_send, k), sv_recv.at[v], peer, (stat_v, 0))
    for k in range(1, blocks):
        vs = lax.rem(v + blocks - k, blocks)
        arrived(stat_v.at[vs], sv_recv.at[vs], (g, partner))
    stats = stat_v[0]
    for n in range(1, blocks):
        stats = stats + stat_v[n]
    stat_g[g] = stats
    for k, peer in enumerate(along_dp):
        go(stat_g.at[g], stat_g.at[g], (sg_send, k), sg_recv.at[g], peer, (stat_g, 0))
    for k in range(1, groups):
        gs = lax.rem(g + groups - k, groups)
        arrived(stat_g.at[gs], sg_recv.at[gs], (g, partner))
    stats = stat_g[0]
    for n in range(1, groups):
        stats = stats + stat_g[n]

    loss, for_q, for_p, q_coef, p_coef = contrast(stats, goal[:, :queries], queries)
    loss_ref[...] = loss

    for_q = [jnp.broadcast_to(y, (queries, lanes)) for y in for_q + [q_coef]]
    for_p = [jnp.broadcast_to(y, (queries, lanes)) for y in for_p + [p_coef]]

    @pl.loop(0, tiles)
    def _(t):
        for n in range(parts):
            at = pl.ds(aligned(t * tile + n * lanes, lanes), lanes)
            rep_q, rep_p = rep[:queries, at], rep[queries:, at]
            grad_q, grad_p = for_q[queries] * rep_q, for_p[queries] * rep_p
            for i in range(queries):
                grad_q = grad_q + for_q[i] * rep_p[i : i + 1]
                grad_p = grad_p + for_p[i] * rep_q[i : i + 1]
            inv[:queries, at] = grad_q * inv[:queries, at]
            inv[queries:, at] = grad_p * inv[queries:, at]
        at = pl.ds(aligned(t * tile, tile), tile)
        first = 0
        for a in range(groups):
            for s in range(seqs):
                size = len_q if s < seq_q else len_p
                row = a * seq_q + s if s < seq_q else queries + a * seq_p + s - seq_q
                sig[first : first + size, at] = (
                    sig[first : first + size, at].astype(jnp.float32) * inv[row : row + 1, at]
                ).astype(sig.dtype)
                first += size

    side = groups // 2
    upper = lax.div(g, side)
    far_base, near_base = lax.rem(upper + 1, 2) * side, upper * side
    if tree:
        stages = [(3, 0), (3, 1), (1, 0), (2, 0), (1, 1), (2, 1), (0, 0), (0, 1)]
    else:
        stages = [(r, h) for r in list(range(1, half)) + [0] for h in range(2)]
    tall = side * rows

    def place(k):
        if k < side:
            return k + (1 - upper) * (side - 1 - 2 * k)
        return lax.rem(g + 1 + k - side, side)

    def group_of(k):
        return (far_base if k < side else near_base) + place(k)

    def chunk(k):
        return pl.ds(aligned(place(k) * rows, rows), rows)

    def hand_over(s):
        go(away.at[s], pair.at[s], (pair_send, s), pair_recv.at[s], (g, partner), (away, s))

    def outcome(s):
        r, h = stages[s]
        arrived(pair.at[s], pair_recv.at[s], (g, partner))
        for k in range(h * side, (h + 1) * side):
            at = chunk(k)
            value = mine[s % 2, at] + pair[s, at].astype(jnp.float32)
            if tree and (r, k % 2) in ((1, 0), (2, 1)):
                arrived(relayed.at[k], relay_recv.at[k], (g, partner))
                value = value + relayed[k].astype(jnp.float32)
            if r:
                pooled[s, at] = value.astype(pooled.dtype)
                sem = (plane_send, s, k % side)
                if tree and r == 3:
                    to = (g, vocab_of(to_chip(2 - k % 2)))
                    go(pooled.at[s, at], relayed.at[k], sem, relay_recv.at[k], to, (relayed, k))
                else:
                    to = (g, vocab_of(to_chip(r)))
                    go(pooled.at[s, at], froms.at[r, k], sem, from_recv.at[r, k], to, (relayed, k))
                continue
            for d in direct:
                arrived(froms.at[d, k], from_recv.at[d, k], (g, partner))
                value = value + froms[d, k].astype(jnp.float32)
            if k < groups - 1:
                turned[k] = value.astype(turned.dtype)
                to = (group_of(k), v)
                go(turned.at[k], last.at[g], (last_send, k), last_recv.at[g], to, (turned, k))
                continue
            for n in range(1, groups):
                gs = lax.rem(g + n, groups)
                arrived(last.at[gs], last_recv.at[gs], (gs, v))
                value = value + last[gs].astype(jnp.float32)
            qo_ref[...] = value[:rows_q].astype(qo_ref.dtype)
            po_ref[...] = value[rows_q:].astype(po_ref.dtype)

    def pick(s, values):
        found = values[0]
        for n in range(1, len(values)):
            found = lax.select(s == n, values[n], found)
        return found

    def gradient(s, ours):
        to = pick(s, [to_chip(r) for r, h in stages]) * 2 + (core if ours else 1 - core)
        base = pick(s, [near_base if h else far_base for r, h in stages])
        return lax.dot_general(
            sig[pl.ds(aligned(base * rows, tall), tall), :stored],
            wv[:stored, pl.ds(aligned(to * width, width), width)],
            (((1,), (0,)), ((), ())),
            preferred_element_type=jnp.float32,
        )

    @pl.loop(0, len(stages))
    def _(s):
        away[s] = gradient(s, False).astype(away.dtype)
        for n in range(len(stages)):

            @pl.when(s == n)
            def _():
                hand_over(n)
                if n:
                    outcome(n - 1)

        mine[lax.rem(s, 2)] = gradient(s, True)

    outcome(len(stages) - 1)
    drain()


def shards(
    query_hidden, passage_hidden_rows, head_weight, head_bias, query_mask, passage_mask, positives
):
    groups, blocks = lax.axis_size("dp"), lax.axis_size("vocab")
    seq_q, len_q = query_mask.shape
    seq_p, len_p = passage_mask.shape
    rows_q = seq_q * len_q
    rows, width = rows_q + seq_p * len_p, query_hidden.shape[1]
    depth, cols = head_weight.shape
    weight = head_weight.T
    if cols % 8:
        weight = jnp.pad(weight, ((0, -cols % 8), (0, 0)))
    tile = min(512, -(-cols // lanes) * lanes)
    tiles = -(-cols // tile)
    padded = tiles * tile
    unroll = 2 if tiles % 2 == 0 else 1
    bias = jnp.pad(head_bias.astype(jnp.float32), (0, padded - cols)).reshape(1, -1)
    queries = groups * seq_q
    seqs = queries + groups * seq_p
    half, side = blocks // 2, groups // 2
    stages = 2 * half
    held = -(-(seq_q + seq_p + 1) // 8) * 8
    everything = groups * rows
    dma, vmem = pltpu.SemaphoreType.DMA, pltpu.VMEM
    inside = pl.BlockSpec(memory_space=pltpu.VMEM)
    anywhere = pl.BlockSpec(memory_space=pl.ANY)
    bf16, f32 = jnp.bfloat16, jnp.float32
    loss, query_grad, passage_grad = pl.pallas_call(
        functools.partial(
            head_kernel, groups, blocks, seq_q, len_q, seq_p, len_p, cols, tile, unroll
        ),
        out_shape=(
            jax.ShapeDtypeStruct((1, 1), f32),
            jax.ShapeDtypeStruct((rows_q, width), bf16),
            jax.ShapeDtypeStruct((rows - rows_q, width), bf16),
        ),
        in_specs=[
            anywhere, anywhere, anywhere, inside, inside, inside,
            pl.BlockSpec(memory_space=pltpu.SMEM),
        ],
        out_specs=(inside, inside, inside),
        scratch_shapes=[
            vmem((everything, depth), bf16),
            vmem((padded, depth), bf16),
            vmem((everything, padded), bf16),
            vmem((everything, lanes), f32),
            vmem((groups, seq_q + seq_p, padded), f32),
            vmem((seqs, padded), f32),
            vmem((seqs, padded), f32),
            vmem((unroll, 2 * rows, tile), f32),
            vmem((held, lanes), jnp.int32),
            vmem((groups, held, lanes), jnp.int32),
            vmem((seqs, lanes), f32),
            vmem((1, lanes), f32),
            vmem((blocks, queries, lanes), f32),
            vmem((groups, queries, lanes), f32),
            vmem((stages, side * rows, width), bf16),
            vmem((stages, side * rows, width), bf16),
            vmem((2, side * rows, width), f32),
            vmem((stages, side * rows, width), bf16),
            vmem((groups, rows, width), bf16),
            vmem((half, groups, rows, width), bf16),
            vmem((groups, rows, width), bf16),
            vmem((groups, rows, width), bf16),
            dma((tiles,)),
            dma((2,)),
            dma((groups,)),
            dma((groups,)),
            dma((groups,)),
            dma((groups, 3 * half + 2)),
            dma((blocks, groups, 2)),
            dma((blocks,)),
            dma((blocks,)),
            dma((groups,)),
            dma((groups,)),
            dma((stages,)),
            dma((stages,)),
            dma((stages, side)),
            dma((groups,)),
            dma((half, groups)),
            dma((groups,)),
            dma((groups,)),
        ],
        compiler_params=pltpu.CompilerParams(
            collective_id=0, has_side_effects=True, vmem_limit_bytes=63 << 20
        ),
    )(
        query_hidden, passage_hidden_rows, weight, bias, query_mask, passage_mask, positives
    )
    return (loss[0, 0], query_grad, passage_grad)


def solution(mesh):
    placed = (
        P("dp", "vocab"),
        P("dp", "vocab"),
        P(None, ("dp", "vocab")),
        P(("dp", "vocab")),
        P("dp", None),
        P("dp", None),
        P("dp"),
    )
    return jax.shard_map(
        shards,
        mesh=mesh,
        in_specs=placed,
        out_specs=(P(), P("dp", "vocab"), P("dp", "vocab")),
        check_vma=False,
    )
```

time: 199 us -> 104 us (0.52)
  local copies, waits for them, and re-layouts: 51.3 us -> 2.91 us
  Pallas kernels: 143 us -> 97.3 us
    pallas_call x5 -> x1, Pallas kernels: 143 us -> 97.3 us  [shards(): pl.pallas_call(functools.partial(head_kernel, groups, blocks, seq_q, len_...]
    unnamed x6 -> x2, local copies, waits for them, and re-layouts: 45.4 us -> 2.91 us
    reshape x8 -> x0, local copies, waits for them, and re-layouts: 5.1 us -> none  [the longest x1 1.31 us: compute_forward(): head_bias.reshape(1, -1)]
    concatenate x2 -> x0, other arithmetic: 2.27 us -> none  [the longest x1 1.54 us: shards(): own = jnp.concatenate((query_hidden, passage_hidden_rows), 0)]
where the time goes in v1:
time: 104 us
  Pallas kernels  97.3 us (94%)
  local copies, waits for them, and re-layouts  2.91 us (3%)
  between operations  2.45 us (2%)
  other arithmetic  1.31 us (1%)
    pallas_call x1, Pallas kernels, shards(): pl.pallas_call(functools.partial(head_kernel, groups, blocks, seq_q, len_...  97.3 us
    unnamed x2, local copies, waits for them, and re-layouts  2.91 us

profile of v1, /device:TPU:0, one launch (start us, length us, event | category | flops | bytes accessed | tf_op | source)
XLA Modules:
  0.0 104.0 jit_solution(7001123681539103595)
XLA Ops:
  0.6 1.3 %pad_convert_fusion = f32[4096]{0:T(1024)} fusion(bf16[4008]{0:T(1024)(128)(2,1)} %param.10), kind=kLoop, calls=%fused_computation | loop fusion | flops 4096 | bytes 24400 | tf_op jit(solution)/shard_map/reshape | solution.py:494
  1.9 97.3 %shard_map.94 = (f32[1,1]{1,0:T(1,128)}, bf16[32,512]{1,0:T(8,128)(2,1)}, bf16[96,512]{1,0:T(8,128)(2,1)}) custom-call(bf16[32,512]{1,0:T(8,128)(2,1)} %q_ref.1, bf16[96,512]{1,0:T(8,128)(2,1)} %p_ref.1, bf16[4008,4096]{1,0:T(8,128)(2,1)} %bitcast.3, f32[1,4096]{1,0:T(1,128)} %bitcast.4, s32[2,16]{1,0:T(2,128)} %qm_ref.1, s32[2,48]{1,0:T(2,128)} %pm_ref.1, ...), custom_call_target="tpu_custom_call" | custom-call | tf_op jit(solution)/shard_map/pallas_call | solution.py:505
  99.9 1.4 %copy.14 = bf16[32,512]{1,0:T(8,128)(2,1)} copy(bf16[32,512]{1,0:T(8,128)(2,1)} %get-tuple-element.13) | data formatting | bytes 65536
  101.3 1.5 %copy.15 = bf16[96,512]{1,0:T(8,128)(2,1)} copy(bf16[96,512]{1,0:T(8,128)(2,1)} %get-tuple-element.14) | data formatting | bytes 196608

commit v2 on v1

--- a/solution.py
+++ b/solution.py
@@ -61,7 +61,7 @@
     tree = half == 4
     rows_q = seq_q * len_q
     rows, width = rows_q + seq_p * len_p, q_ref.shape[1]
-    queries, tiles = groups * seq_q, x.shape[1] and sig.shape[1] // tile
+    queries, tiles = groups * seq_q, sig.shape[1] // tile
     seqs = seq_q + seq_p
 
     def to_chip(r):
@@ -106,28 +106,23 @@
         at = pl.ds(t * tile, n)
         loads.append(pltpu.make_async_copy(w_ref.at[at], wv.at[at], w_sem.at[t]))
 
-    def block(vs, gs, part=None):
-        n = rows if part is None else rows // 2
+    def block(vs, gs, part=None, count=1):
+        n = rows * count if part is None else rows * count // 2
         at = gs * rows if part is None else gs * rows + part * n
-        return x.at[
-            pl.ds(aligned(at, n), n), pl.ds(aligned(vs * width, width), width)
-        ]
-
-    full = (x, pl.ds(0, rows), pl.ds(0, width))
-    part_of = (x, pl.ds(0, rows // 2), pl.ds(0, width))
-    own_cols = pl.ds(aligned(v * width, width), width)
+        return x.at[vs, pl.ds(aligned(at, rows // 2), n)]
+
+    full = lambda count: (x, 0, pl.ds(0, rows * count))
+    part_of = lambda count: (x, 0, pl.ds(0, rows * count // 2))
     own_q = pltpu.make_async_copy(
-        q_ref, x.at[pl.ds(aligned(g * rows, rows), rows_q), own_cols], own_sem.at[0]
+        q_ref, x.at[v, pl.ds(aligned(g * rows, rows), rows_q)], own_sem.at[0]
     )
     own_p = pltpu.make_async_copy(
         p_ref,
-        x.at[pl.ds(aligned(g * rows + rows_q, rows_q), rows - rows_q), own_cols],
+        x.at[v, pl.ds(aligned(g * rows + rows_q, rows_q), rows - rows_q)],
         own_sem.at[1],
     )
     own_q.start()
     own_p.start()
-    for load in loads:
-        load.start()
 
     along_dp = [(lax.rem(g + k, groups), v) for k in range(1, groups)]
     along_vocab = [(g, lax.rem(v + k, blocks)) for k in range(1, blocks)]
@@ -153,53 +148,56 @@
         order += [base, base + 1]
 
     direct = [1, 2] if tree else list(range(1, half))
+    units = [(order[0], 1), (order[1], 1)] + [(base, 2) for base in bases[1:]]
 
     def fan(n):
-        gs = order[n]
+        gs, c = units[n]
+        mine_at = block(v, gs, None, c)
         for k, r in enumerate(direct):
-            vs = vocab_of(to_chip(r))
-            go(block(v, gs), block(v, gs), (x_send, n, k), x_recv.at[v, gs, 0], (g, vs), full)
-        sem = (x_send, n, half)
-        go(block(v, gs), block(v, gs), sem, x_recv.at[v, gs, 0], (g, partner), full)
+            to = (g, vocab_of(to_chip(r)))
+            go(mine_at, mine_at, (x_send, n, k), x_recv.at[v, gs, 0], to, full(c))
+        to = (g, partner)
+        go(mine_at, mine_at, (x_send, n, half), x_recv.at[v, gs, 1], to, full(c))
 
     def relay(n):
-        gs = order[n]
+        gs, c = units[n]
         for k, r in enumerate(direct):
             vs = vocab_of(from_chip(r))
-            arrived(block(vs, gs), x_recv.at[vs, gs, 0], (g, partner))
+            whole = block(vs, gs, None, c)
+            arrived(whole, x_recv.at[vs, gs, 0], (g, partner))
             if tree:
                 to = (g, vocab_of(to_chip(3 - r)))
-                part = block(vs, gs, k)
-                go(part, part, (x_send, n, half + 1 + k), x_recv.at[vs, gs, k], to, part_of)
-            go(
-                block(vs, gs), block(vs, gs), (x_send, n, len(direct) + 3 + half + k),
-                x_recv.at[vs, gs, 0], (g, partner), full,
-            )
+                part = block(vs, gs, k, c)
+                sem = (x_send, n, half + 1 + k)
+                go(part, part, sem, x_recv.at[vs, gs, k], to, part_of(c))
+            sem = (x_send, n, len(direct) + 3 + half + k)
+            go(whole, whole, sem, x_recv.at[vs, gs, 0], (g, partner), full(c))
 
     def corner(n):
         if not tree:
             return
-        gs, vs = order[n], vocab_of(to_chip(3))
+        (gs, c), vs = units[n], vocab_of(to_chip(3))
         for k in range(2):
-            part = block(vs, gs, k)
+            part = block(vs, gs, k, c)
             arrived(part, x_recv.at[vs, gs, k], (g, partner))
             sem = (x_send, n, half + 3 + k)
-            go(part, part, sem, x_recv.at[vs, gs, k], (g, partner), part_of)
+            go(part, part, sem, x_recv.at[vs, gs, k], (g, partner), part_of(c))
 
     def settled(n):
-        gs = order[n]
+        gs, c = units[n]
         for r in range(half):
             vs = from_chip(r) * 2 + 1 - core
             if tree and r == 3:
                 for k in range(2):
-                    arrived(block(vs, gs, k), x_recv.at[vs, gs, k], (g, partner))
+                    arrived(block(vs, gs, k, c), x_recv.at[vs, gs, k], (g, partner))
             else:
-                arrived(block(vs, gs), x_recv.at[vs, gs, 0], (g, partner))
+                sem = x_recv.at[vs, gs, 0 if r else 1]
+                arrived(block(vs, gs, None, c), sem, (g, partner))
 
     own_q.wait()
     own_p.wait()
     for n in range(1, groups):
-        go(block(v, g), block(v, g), (z_send, n - 1), x_recv.at[v, g, 0], (order[n], v), full)
+        go(block(v, g), block(v, g), (z_send, n - 1), x_recv.at[v, g, 0], (order[n], v), full(1))
         if n == 1:
             fan(0)
     for n in range(1, groups):
@@ -207,14 +205,24 @@
         go(smalls.at[g], smalls.at[g], sem, small_recv.at[g], (order[n], v), (smalls, 0))
 
     def reach(n):
-        arrived(block(v, order[n]), x_recv.at[v, order[n], 0], (g, partner))
+        gs, c = units[n]
+        for m in range(c):
+            arrived(block(v, gs + m), x_recv.at[v, gs + m, 0], (g, partner))
         fan(n)
 
+    def fetch(n):
+        for load in loads[n * tiles // 4 : (n + 1) * tiles // 4]:
+            load.start()
+
+    fetch(0)
     reach(1)
+    fetch(1)
     relay(0)
+    fetch(2)
     relay(1)
-    for n in range(2, groups):
+    for n in range(2, len(units)):
         reach(n)
+    fetch(3)
 
     for n in range(1, groups):
         gs = order[n]
@@ -246,8 +254,9 @@
     some = 2 * rows
 
     def product(base, t, slot):
+        at = pl.ds(aligned(base * rows, some), some)
         acc[slot] = lax.dot_general(
-            x[pl.ds(aligned(base * rows, some), some)],
+            jnp.concatenate([x[n, at] for n in range(blocks)], axis=1),
             wv[pl.ds(aligned(t * tile, tile), tile)],
             (((1,), (1,)), ((), ())),
             preferred_element_type=jnp.float32,
@@ -280,8 +289,7 @@
     for k, base in enumerate(bases):
         events = []
         if k + 1 < pairs:
-            a, b = 2 * k + 2, 2 * k + 3
-            events = [(relay, a), (relay, b), (corner, a), (corner, b)]
+            events = [(1, relay), (2, corner)]
 
         @pl.loop(0, rounds)
         def _(i):
@@ -300,17 +308,16 @@
                     pool(base, jnp.maximum(t - 1, 0), (u - 1) % unroll)
                 else:
                     pool(base, t, u)
-            for e, (event, n) in enumerate(events):
-
-                @pl.when(i == min(e, rounds - 1))
+            for at, event in events:
+
+                @pl.when(i == min(at, rounds - 1))
                 def _():
-                    event(n)
+                    event(k + 2)
 
         if unroll > 1:
             pool(base, tiles - 1, unroll - 1)
         if k + 1 < pairs:
-            settled(2 * k + 2)
-            settled(2 * k + 3)
+            settled(k + 2)
 
     parts = tile // lanes
     fold = lambda y: sum(y[:, n * lanes : (n + 1) * lanes] for n in range(parts))
@@ -517,7 +524,7 @@
         ],
         out_specs=(inside, inside, inside),
         scratch_shapes=[
-            vmem((everything, depth), bf16),
+            vmem((blocks, everything, width), bf16),
             vmem((padded, depth), bf16),
             vmem((everything, padded), bf16),
             vmem((everything, lanes), f32),
@@ -559,7 +566,7 @@
             dma((groups,)),
         ],
         compiler_params=pltpu.CompilerParams(
-            collective_id=0, has_side_effects=True, vmem_limit_bytes=63 << 20
+            collective_id=0, has_side_effects=True, vmem_limit_bytes=58 << 20
         ),
     )(
         query_hidden, passage_hidden_rows, weight, bias, query_mask, passage_mask, positives

time: 104 us -> 98 us (0.942)
  Pallas kernels: 97.3 us -> 91 us
    pallas_call x1, Pallas kernels: 97.3 us -> 91 us  [shards(): pl.pallas_call(functools.partial(head_kernel, groups, blocks, seq_q, len_...]
where the time goes in v2:
time: 98 us; the launch traced here: 97.7 us
  Pallas kernels  91 us (93%)
  local copies, waits for them, and re-layouts  2.91 us (3%)
  between operations  2.45 us (3%)
  other arithmetic  1.31 us (1%)
    pallas_call x1, Pallas kernels, shards(): pl.pallas_call(functools.partial(head_kernel, groups, blocks, seq_q, len_...  91 us
    unnamed x2, local copies, waits for them, and re-layouts  2.91 us

profile of v2, /device:TPU:0, one launch (start us, length us, event | category | flops | bytes accessed | tf_op | source)
XLA Modules:
  0.0 97.7 jit_solution(6076854800231933541)
XLA Ops:
  0.6 1.3 %pad_convert_fusion = f32[4096]{0:T(1024)} fusion(bf16[4008]{0:T(1024)(128)(2,1)} %param.10), kind=kLoop, calls=%fused_computation | loop fusion | flops 4096 | bytes 24400 | tf_op jit(solution)/shard_map/reshape | solution.py:501
  1.9 91.0 %shard_map.94 = (f32[1,1]{1,0:T(1,128)}, bf16[32,512]{1,0:T(8,128)(2,1)}, bf16[96,512]{1,0:T(8,128)(2,1)}) custom-call(bf16[32,512]{1,0:T(8,128)(2,1)} %q_ref.1, bf16[96,512]{1,0:T(8,128)(2,1)} %p_ref.1, bf16[4008,4096]{1,0:T(8,128)(2,1)} %bitcast.3, f32[1,4096]{1,0:T(1,128)} %bitcast.4, s32[2,16]{1,0:T(2,128)} %qm_ref.1, s32[2,48]{1,0:T(2,128)} %pm_ref.1, ...), custom_call_target="tpu_custom_call" | custom-call | tf_op jit(solution)/shard_map/pallas_call | solution.py:512
  93.6 1.4 %copy.14 = bf16[32,512]{1,0:T(8,128)(2,1)} copy(bf16[32,512]{1,0:T(8,128)(2,1)} %get-tuple-element.13) | data formatting | bytes 65536
  95.0 1.5 %copy.15 = bf16[96,512]{1,0:T(8,128)(2,1)} copy(bf16[96,512]{1,0:T(8,128)(2,1)} %get-tuple-element.14) | data formatting | bytes 196608
